TPU v7x, 32 devices: a whole 2x2x4 slice. The times are simulated.
32 devices in a mesh: gx: 8 (over z, x), yz: 4 (over y, core).
Axes of the slice: x: 2, y: 2, z: 4, core: 2. Of those that a mesh axis runs over, the one named last changes fastest.
Arguments:
- state: float32 [4, 256, 192, 256], P(None, 'gx', 'yz'), may hold values from -6 to 6
- mean_flow: float32 [256, 192, 256], P('gx', 'yz'), may hold values from 0.2 to 1.2
- face_cell: int32 [6144], P(('gx', 'yz')), may hold values from 0 to 12582911, as said below
- face_normal: float32 [3, 6144], P(None, ('gx', 'yz')), may hold values from -3 to 3
- face_pos: float32 [3, 6144], P(None, ('gx', 'yz')), may hold values from -2 to 2
- observer_pos: float32 [3, 512], replicated, may hold values from 4 to 12
- time_bin: int32 [6144, 512], P(('gx', 'yz')), may hold values from 0 to 63
Outputs:
- state_next: float32 [4, 256, 192, 256], P(None, 'gx', 'yz')
- signal: float32 [512, 64], P(('gx', 'yz'))
Inputs may be any that keep to these rules, and one draw needn't show every extreme that they name: `face_cell`: face j is held by device j // 192 of gx+yz, and its cell, numbered (x 192 + y) * 256 + z, lies in that device's block of grid cells.
All inputs are finite; a program needn't handle non-finite values.
Results may differ from a plain program's by a relative error of at most 0.000084.
Values sent between devices are 32-bit elements; how exact they have to be, the bound alone decides.
A program may use at most 192 MiB of HBM per device.

v0:
```python
import jax
import jax.numpy as jnp
from jax import lax
from jax.sharding import PartitionSpec as P

BINS = 64
time_step = 0.25
four_pi = 4.0 * 3.141592653589793
highest = lax.Precision.HIGHEST


def extended(block, sides, width):
    for axis, dim in sides:
        count = lax.axis_size(axis)
        forward = [(i, i + 1) for i in range(count - 1)]
        backward = [(target, source) for source, target in forward]
        low = lax.ppermute(
            lax.slice_in_dim(block, block.shape[dim] - width, None, axis=dim), axis, forward
        )
        high = lax.ppermute(lax.slice_in_dim(block, 0, width, axis=dim), axis, backward)
        block = jnp.concatenate([low, block, high], axis=dim)
    return block


def diagonals(count):
    index = jnp.arange(count)
    third = jnp.full((count,), 1.0 / 3.0, jnp.float32)
    quarter = jnp.float32(0.25)
    lower = jnp.where(index == 1, quarter, third)
    lower = jnp.where(index == count - 2, quarter, lower)
    lower = jnp.where(index == count - 1, jnp.float32(2.0), lower)
    lower = jnp.where(index == 0, jnp.float32(0.0), lower)
    upper = jnp.where(index == 1, quarter, third)
    upper = jnp.where(index == count - 2, quarter, upper)
    upper = jnp.where(index == 0, jnp.float32(2.0), upper)
    upper = jnp.where(index == count - 1, jnp.float32(0.0), upper)
    return (lower, jnp.ones((count,), jnp.float32), upper)


def inverse_of(lower, middle, upper):
    count = middle.shape[0]
    return lax.linalg.tridiagonal_solve(lower, middle, upper, jnp.eye(count, dtype=jnp.float32))


def compact_rhs(field, axis):
    count = field.shape[axis]
    widths = [(2, 2) if dimension == axis else (0, 0) for dimension in range(field.ndim)]
    padded = jnp.pad(field, widths)

    def take(first, last):
        return lax.slice_in_dim(padded, first, last, axis=axis)

    def plane(index):
        return lax.slice_in_dim(field, index, index + 1, axis=axis)

    inner = 7.0 / 9.0 * (take(3, count + 3) - take(1, count + 1)) + 1.0 / 36.0 * (
        take(4, count + 4) - take(0, count)
    )
    first_row = 0.5 * (4.0 * plane(1) + plane(2) - 5.0 * plane(0))
    second_row = 0.75 * (plane(2) - plane(0))
    before_last = 0.75 * (plane(count - 1) - plane(count - 3))
    last_row = 0.5 * (5.0 * plane(count - 1) - 4.0 * plane(count - 2) - plane(count - 3))
    middle_rows = lax.slice_in_dim(inner, 2, count - 2, axis=axis)
    return jnp.concatenate([first_row, second_row, middle_rows, before_last, last_row], axis)


def explicit_y(padded, count):

    def take(shift):
        return lax.slice_in_dim(padded, 3 + shift, 3 + shift + count, axis=2)

    return (
        0.75 * (take(1) - take(-1))
        - 0.15 * (take(2) - take(-2))
        + 1.0 / 60.0 * (take(3) - take(-3))
    )


def transposed_x(fields):
    part = lax.all_to_all(fields, "gx", split_axis=2, concat_axis=1, tiled=True)
    inverse = inverse_of(*diagonals(part.shape[1]))
    rhs = compact_rhs(part, 1)
    solved = jnp.einsum("ij,fjab->fiab", inverse, rhs, precision=highest)
    return lax.all_to_all(solved, "gx", split_axis=1, concat_axis=2, tiled=True)


def per_device(state, mean_flow, face_cell, face_normal, face_pos, observer_pos, time_bin):
    cells, width, depth = (state.shape[1], state.shape[2], state.shape[3])
    fields = jnp.concatenate([state, mean_flow[None]], 0)
    x_rates = transposed_x(fields)
    crossing = extended(fields[0::2], (("yz", 2),), 3)
    y_rates = explicit_y(crossing, width)
    z_fields = jnp.concatenate([fields[0:1], fields[3:5]], 0)
    z_inverse = inverse_of(*diagonals(depth))
    z_rates = jnp.dot(compact_rhs(z_fields, 3), z_inverse.T, precision=highest)
    pressure, stream, lateral, vertical = (state[0], state[1], state[2], state[3])
    pressure_rate = -(mean_flow * x_rates[0] + x_rates[1] + y_rates[1] + z_rates[1])
    stream_rate = -(
        mean_flow * x_rates[1]
        + stream * x_rates[4]
        + lateral * y_rates[2]
        + vertical * z_rates[2]
        + x_rates[0]
    )
    lateral_rate = -(mean_flow * x_rates[2] + y_rates[0])
    vertical_rate = -(mean_flow * x_rates[3] + z_rates[0])
    rates = jnp.stack([pressure_rate, stream_rate, lateral_rate, vertical_rate])
    state_next = state + time_step * rates
    planes = width * lax.axis_size("yz")
    block = lax.axis_index("gx")
    group = lax.axis_index("yz")
    along_x = face_cell // (planes * depth) - block * cells
    along_y = face_cell // depth % planes - group * width
    along_z = face_cell % depth
    local_cell = (along_x * width + along_y) * depth + along_z
    face_rates = rates.reshape(4, -1)[:, local_cell]
    face_pressure = state_next[0].reshape(-1)[local_cell]
    normal_rate = (
        face_normal[0] * face_rates[1]
        + face_normal[1] * face_rates[2]
        + face_normal[2] * face_rates[3]
    )
    offset_x = observer_pos[0][None, :] - face_pos[0][:, None]
    offset_y = observer_pos[1][None, :] - face_pos[1][:, None]
    offset_z = observer_pos[2][None, :] - face_pos[2][:, None]
    distance = jnp.sqrt(offset_x * offset_x + offset_y * offset_y + offset_z * offset_z)
    normal_r = (
        face_normal[0][:, None] * offset_x
        + face_normal[1][:, None] * offset_y
        + face_normal[2][:, None] * offset_z
    ) / distance
    contribution = (
        normal_rate[:, None]
        + (face_rates[0][:, None] + face_pressure[:, None] / distance) * normal_r
    ) / (four_pi * distance)
    onehot = (time_bin[:, :, None] == jnp.arange(BINS, dtype=jnp.int32)).astype(jnp.float32)
    signal = lax.psum_scatter(
        jnp.sum(contribution[:, :, None] * onehot, axis=0),
        ("gx", "yz"),
        scatter_dimension=0,
        tiled=True,
    )
    return (state_next, signal)


def solution(mesh):
    in_specs = (
        P(None, "gx", "yz", None),
        P("gx", "yz", None),
        P(("gx", "yz")),
        P(None, ("gx", "yz")),
        P(None, ("gx", "yz")),
        P(),
        P(("gx", "yz"), None),
    )
    out_specs = (P(None, "gx", "yz", None), P(("gx", "yz"), None))
    return jax.shard_map(
        per_device, mesh=mesh, in_specs=in_specs, out_specs=out_specs, check_vma=False
    )
```

profile of v0, /device:TPU:0, one launch (start us, length us, event | category | flops | bytes accessed | tf_op | source)
XLA Modules:
  0.0 1276.9 jit_solution(14212559706522243462)
XLA Ops:
  31.2 458.7 %while.8 = (s32[]{:T(128)}, f32[]{:T(128)}, f32[256]{0:T(256)S(1)}, f32[7,32]{1,0:T(8,128)S(1)}, f32[7,32,256]{2,1,0:T(8,128)S(1)}, /*index=5*/f32[7,32]{1,0:T(8...) while((s32[]{:T(128)}, f32[]{:T(128)}, ...), condition=%wide.region_1.2_spmd, body=%wide.region_0.1_spmd.sunk | while | flops 24705 | bytes 269033 | solution.py:42
  74.5 20.3 %subtract_divide_fusion.125 = (f32[256]{0:T(256)S(1)}, f32[256]{0:T(256)S(1)}, f32[256]{0:T(256)S(1)}, f32[256]{0:T(256)S(1)}, f32[256]{0:T(256)S(1)}, /*index=5...) fusion(f32[256]{0:T(256)S(1)} %bitcast.1217, ...), kind=kLoop, calls=%fused_computation.37.clone.1 | loop fusion | flops 24576 | bytes 66816 | tf_op jit(solution)/shard_map/while/body/eval_jaxpr/div | solution.py:42
  140.0 20.3 %subtract_divide_fusion.125 = (f32[256]{0:T(256)S(1)}, f32[256]{0:T(256)S(1)}, f32[256]{0:T(256)S(1)}, f32[256]{0:T(256)S(1)}, f32[256]{0:T(256)S(1)}, /*index=5...) fusion(f32[256]{0:T(256)S(1)} %bitcast.1217, ...), kind=kLoop, calls=%fused_computation.37.clone.1 | loop fusion | flops 24576 | bytes 66816 | tf_op jit(solution)/shard_map/while/body/eval_jaxpr/div | solution.py:42
  205.5 20.3 %subtract_divide_fusion.125 = (f32[256]{0:T(256)S(1)}, f32[256]{0:T(256)S(1)}, f32[256]{0:T(256)S(1)}, f32[256]{0:T(256)S(1)}, f32[256]{0:T(256)S(1)}, /*index=5...) fusion(f32[256]{0:T(256)S(1)} %bitcast.1217, ...), kind=kLoop, calls=%fused_computation.37.clone.1 | loop fusion | flops 24576 | bytes 66816 | tf_op jit(solution)/shard_map/while/body/eval_jaxpr/div | solution.py:42
  271.0 20.3 %subtract_divide_fusion.125 = (f32[256]{0:T(256)S(1)}, f32[256]{0:T(256)S(1)}, f32[256]{0:T(256)S(1)}, f32[256]{0:T(256)S(1)}, f32[256]{0:T(256)S(1)}, /*index=5...) fusion(f32[256]{0:T(256)S(1)} %bitcast.1217, ...), kind=kLoop, calls=%fused_computation.37.clone.1 | loop fusion | flops 24576 | bytes 66816 | tf_op jit(solution)/shard_map/while/body/eval_jaxpr/div | solution.py:42
  336.6 20.3 %subtract_divide_fusion.125 = (f32[256]{0:T(256)S(1)}, f32[256]{0:T(256)S(1)}, f32[256]{0:T(256)S(1)}, f32[256]{0:T(256)S(1)}, f32[256]{0:T(256)S(1)}, /*index=5...) fusion(f32[256]{0:T(256)S(1)} %bitcast.1217, ...), kind=kLoop, calls=%fused_computation.37.clone.1 | loop fusion | flops 24576 | bytes 66816 | tf_op jit(solution)/shard_map/while/body/eval_jaxpr/div | solution.py:42
  402.1 20.3 %subtract_divide_fusion.125 = (f32[256]{0:T(256)S(1)}, f32[256]{0:T(256)S(1)}, f32[256]{0:T(256)S(1)}, f32[256]{0:T(256)S(1)}, f32[256]{0:T(256)S(1)}, /*index=5...) fusion(f32[256]{0:T(256)S(1)} %bitcast.1217, ...), kind=kLoop, calls=%fused_computation.37.clone.1 | loop fusion | flops 24576 | bytes 66816 | tf_op jit(solution)/shard_map/while/body/eval_jaxpr/div | solution.py:42
  467.6 20.3 %subtract_divide_fusion.125 = (f32[256]{0:T(256)S(1)}, f32[256]{0:T(256)S(1)}, f32[256]{0:T(256)S(1)}, f32[256]{0:T(256)S(1)}, f32[256]{0:T(256)S(1)}, /*index=5...) fusion(f32[256]{0:T(256)S(1)} %bitcast.1217, ...), kind=kLoop, calls=%fused_computation.37.clone.1 | loop fusion | flops 24576 | bytes 66816 | tf_op jit(solution)/shard_map/while/body/eval_jaxpr/div | solution.py:42
  529.7 19.0 %subtract_divide_fusion.32 = (f32[256]{0:T(256)S(1)}, f32[256]{0:T(256)S(1)}, f32[256]{0:T(256)S(1)}, f32[256]{0:T(256)S(1)}, f32[256]{0:T(256)S(1)}, /*index=5*...) fusion(f32[256]{0:T(256)S(1)} %bitcast.1418, ...), kind=kLoop, calls=%fused_computation.305 | loop fusion | flops 23808 | bytes 64760 | tf_op jit(solution)/shard_map/eval_jaxpr/div | solution.py:42
  551.3 151.0 %while.9 = (s32[]{:T(128)}, f32[256]{0:T(256)S(1)}, f32[7,32,256]{2,1,0:T(8,128)S(1)}, f32[7,32,256]{2,1,0:T(8,128)S(1)}, f32[7,32]{1,0:T(8,128)S(1)}, /*index=5...) while((s32[]{:T(128)}, f32[256]{0:T(256)S(1)}, ...), condition=%wide.region_3.4_spmd, body=%wide.region_2.3_spmd.sunk | while | flops 16418 | bytes 266713 | solution.py:42
  553.0 19.7 %multiply_subtract_fusion.125 = (f32[256]{0:T(256)S(1)}, f32[256]{0:T(256)S(1)}, f32[256]{0:T(256)S(1)}, f32[256]{0:T(256)S(1)}, f32[256]{0:T(256)S(1)}, /*index...) fusion(f32[256]{0:T(256)S(1)} %bitcast.1266, ...), kind=kLoop, calls=%fused_computation.103.clone.1 | loop fusion | flops 16384 | bytes 66688 | tf_op jit(solution)/shard_map/while/body/eval_jaxpr/sub | solution.py:42
  574.6 19.7 %multiply_subtract_fusion.125 = (f32[256]{0:T(256)S(1)}, f32[256]{0:T(256)S(1)}, f32[256]{0:T(256)S(1)}, f32[256]{0:T(256)S(1)}, f32[256]{0:T(256)S(1)}, /*index...) fusion(f32[256]{0:T(256)S(1)} %bitcast.1266, ...), kind=kLoop, calls=%fused_computation.103.clone.1 | loop fusion | flops 16384 | bytes 66688 | tf_op jit(solution)/shard_map/while/body/eval_jaxpr/sub | solution.py:42
  596.1 19.7 %multiply_subtract_fusion.125 = (f32[256]{0:T(256)S(1)}, f32[256]{0:T(256)S(1)}, f32[256]{0:T(256)S(1)}, f32[256]{0:T(256)S(1)}, f32[256]{0:T(256)S(1)}, /*index...) fusion(f32[256]{0:T(256)S(1)} %bitcast.1266, ...), kind=kLoop, calls=%fused_computation.103.clone.1 | loop fusion | flops 16384 | bytes 66688 | tf_op jit(solution)/shard_map/while/body/eval_jaxpr/sub | solution.py:42
  617.7 19.7 %multiply_subtract_fusion.125 = (f32[256]{0:T(256)S(1)}, f32[256]{0:T(256)S(1)}, f32[256]{0:T(256)S(1)}, f32[256]{0:T(256)S(1)}, f32[256]{0:T(256)S(1)}, /*index...) fusion(f32[256]{0:T(256)S(1)} %bitcast.1266, ...), kind=kLoop, calls=%fused_computation.103.clone.1 | loop fusion | flops 16384 | bytes 66688 | tf_op jit(solution)/shard_map/while/body/eval_jaxpr/sub | solution.py:42
  639.2 19.7 %multiply_subtract_fusion.125 = (f32[256]{0:T(256)S(1)}, f32[256]{0:T(256)S(1)}, f32[256]{0:T(256)S(1)}, f32[256]{0:T(256)S(1)}, f32[256]{0:T(256)S(1)}, /*index...) fusion(f32[256]{0:T(256)S(1)} %bitcast.1266, ...), kind=kLoop, calls=%fused_computation.103.clone.1 | loop fusion | flops 16384 | bytes 66688 | tf_op jit(solution)/shard_map/while/body/eval_jaxpr/sub | solution.py:42
  660.8 19.7 %multiply_subtract_fusion.125 = (f32[256]{0:T(256)S(1)}, f32[256]{0:T(256)S(1)}, f32[256]{0:T(256)S(1)}, f32[256]{0:T(256)S(1)}, f32[256]{0:T(256)S(1)}, /*index...) fusion(f32[256]{0:T(256)S(1)} %bitcast.1266, ...), kind=kLoop, calls=%fused_computation.103.clone.1 | loop fusion | flops 16384 | bytes 66688 | tf_op jit(solution)/shard_map/while/body/eval_jaxpr/sub | solution.py:42
  682.4 19.7 %multiply_subtract_fusion.125 = (f32[256]{0:T(256)S(1)}, f32[256]{0:T(256)S(1)}, f32[256]{0:T(256)S(1)}, f32[256]{0:T(256)S(1)}, f32[256]{0:T(256)S(1)}, /*index...) fusion(f32[256]{0:T(256)S(1)} %bitcast.1266, ...), kind=kLoop, calls=%fused_computation.103.clone.1 | loop fusion | flops 16384 | bytes 66688 | tf_op jit(solution)/shard_map/while/body/eval_jaxpr/sub | solution.py:42
  702.3 19.1 %multiply_subtract_fusion.32 = (f32[256]{0:T(256)S(1)}, f32[256]{0:T(256)S(1)}, f32[256]{0:T(256)S(1)}, f32[256]{0:T(256)S(1)}, f32[256]{0:T(256)S(1)}, /*index=...) fusion(f32[256]{0:T(256)S(1)} %bitcast.1364, ...), kind=kLoop, calls=%fused_computation.274 | loop fusion | flops 15872 | bytes 64636 | tf_op jit(solution)/shard_map/eval_jaxpr/sub | solution.py:42
  729.3 9.1 copy.197
  740.1 25.2 %pad_slice_fusion.3 = (f32[5,256,6,256]{1,3,2,0:T(8,128)}, f32[5,256,6,256]{1,3,2,0:T(8,128)}, f32[5,256,6,256]{1,3,2,0:T(8,128)}, f32[5,256,6,256]{1,3,2,0:T(8,128)}) fusion(f32[5,256,6,256]{1,3,2,0:T(8,128)} %copy.197), kind=kLoop, calls=%fused_computation.140 | loop fusion | bytes 39321600 | tf_op jit(solution)/shard_map/slice | solution.py:51
  775.4 16.3 %fusion.1 = f32[5,252,6,256]{1,3,2,0:T(8,128)} fusion(f32[5,256,6,256]{1,3,2,0:T(8,128)} %get-tuple-element.521, f32[5,256,6,256]{1,3,2,0:T(8,128)} %get-tuple-element.520, f32[5,256,6,256]{1,3,2,0:T(8,128)} %get-tuple-element.519, f32[5,256,6,256]{1,3,2,0:T(8,128)} %get-tuple-element.518), kind=kLoop, calls=%fused_computation.157 | loop fusion | flops 9676800 | bytes 38707200 | tf_op jit(solution)/shard_map/add | solution.py:56
  791.7 17.8 %concatenate.55 = f32[5,256,6,256]{1,3,2,0:T(8,128)} concatenate(f32[5,1,6,256]{1,3,2,0:T(8,128)} %copy.198, f32[5,1,6,256]{1,3,2,0:T(8,128)} %copy.199, f32[5,252,6,256]{1,3,2,0:T(8,128)} %fusion.1, f32[5,1,6,256]{1,3,2,0:T(8,128)} %copy.200, f32[5,1,6,256]{1,3,2,0:T(8,128)} %copy.201), dimensions={1} | concatenate | bytes 15728640 | tf_op jit(solution)/shard_map/concatenate | solution.py:64
  809.4 10.5 convolution_bitcast_fusion
  820.0 10.4 copy.202
  894.6 9.5 fusion.5
  904.1 11.4 concatenate.62
  937.4 11.6 fusion.68
  948.9 11.3 fusion.69
  960.2 35.8 %fusion.8 = f32[3,32,48,256]{3,2,1,0:T(8,128)} fusion(f32[3,32,48,256]{3,1,2,0:T(8,128)} %get-tuple-element.529, f32[3,32,48,256]{3,1,2,0:T(8,128)} %get-tuple-element.526, f32[3,32,48,256]{3,1,2,0:T(8,128)} %get-tuple-element.528, f32[3,32,48,256]{3,1,2,0:T(8,128)} %get-tuple-element.525, f32[3,32,48,256]{3,1,2,0:T(8,128)} %get-tuple-element.527, ...), kind=kLoop, calls=%fused_computation.176 | loop fusion | flops 9437184 | bytes 33030144 | tf_op jit(solution)/shard_map/add | solution.py:73
  996.0 67.9 %all-to-all-done.1 = f32[5,256,6,256]{3,2,0,1:T(8,128)} async-done(((f32[5,256,6,256]{3,2,0,1:T(8,128)}), f32[5,256,6,256]{3,2,0,1:T(8,128)}, u32[]{:S(2)}, u32[]{:S(2)}) %all-to-all-start.1) | async-done | bytes 7864352 | tf_op jit(solution)/shard_map/all_to_all | solution.py:84
  1077.6 11.4 fusion.30
  1135.0 134.8 %reduce-scatter.4.cloned.1.call-done = f32[16,64]{1,0:T(8,128)} async-done(((f32[512,64]{1,0:T(8,128)}), f32[16,64]{1,0:T(8,128)}) %reduce-scatter.4.cloned.1.call-update) | async-done | bytes 4112
  (282 shorter events, 233.5 us)
Async XLA Ops:
  11.1 3.1 copy-start
  21.8 699.7 %all-to-all-start = ((f32[5,32,48,256]{3,1,0,2:T(8,128)}), f32[5,32,48,256]{3,1,0,2:T(8,128)}, u32[]{:S(2)}, u32[]{:S(2)}) async-start(f32[5,32,48,256]{3,1,0,2:T(8,128)} %copy.194), calls=%async_computation | async-start | bytes 15728640 | tf_op jit(solution)/shard_map/all_to_all | solution.py:80
  830.4 233.5 %all-to-all-start.1 = ((f32[5,256,6,256]{3,2,0,1:T(8,128)}), f32[5,256,6,256]{3,2,0,1:T(8,128)}, u32[]{:S(2)}, u32[]{:S(2)}) async-start(f32[5,256,6,256]{3,2,0,1:T(8,128)} %copy.202), calls=%async_computation.1 | async-start | bytes 20971520 | tf_op jit(solution)/shard_map/all_to_all | solution.py:84
  836.4 433.4 %reduce-scatter.4.cloned.1.call-start = ((), (), s32[]{:S(2)}) async-start(), calls=%async_computation.3 | async-start | bytes 270336
  839.1 6.7 copy-start.1
  839.1 6.7 copy-start.3
  840.1 85.1 %collective-permute-start.1 = (f32[3,32,3,256]{3,1,2,0:T(8,128)}, f32[3,32,3,256]{3,1,2,0:T(8,128)}, u32[]{:S(2)}, u32[]{:S(2)}) collective-permute-start(f32[3,32,3,256]{3,1,2,0:T(8,128)} %copy.285), channel_id=1, source_target_pairs={{0,1},{1,2},{2,3},{4,5},{5,6},{6,7},{8,9},{9,10},{10,11},{12,13},{... | collective-permute-start | bytes 884744 | tf_op jit(solution)/shard_map/ppermute | solution.py:17
  843.0 92.7 %collective-permute-start = (f32[3,32,3,256]{3,1,2,0:T(8,128)}, f32[3,32,3,256]{3,1,2,0:T(8,128)}, u32[]{:S(2)}, u32[]{:S(2)}) collective-permute-start(f32[3,32,3,256]{3,1,2,0:T(8,128)} %copy.286), channel_id=1, source_target_pairs={{1,0},{2,1},{3,2},{5,4},{6,5},{7,6},{9,8},{10,9},{11,10},{13,12},{... | collective-permute-start | bytes 884744 | tf_op jit(solution)/shard_map/ppermute | solution.py:20
  845.8 2.2 copy-start.2
  904.1 11.4 copy-start.14
  904.1 11.5 copy-start.12
  904.1 11.5 copy-start.13
  916.2 8.3 copy-start.8
  1063.9 11.3 slice-start.4
  1070.5 4.7 slice-start.2
  1070.5 4.7 slice-start.5
  1071.9 3.3 slice-start
  1071.9 4.6 slice-start.3
  1072.3 4.9 slice-start.1
  1072.3 5.3 copy-start.4
  1120.9 2.7 copy-start.5
  1123.6 2.6 copy-start.7
  1123.6 2.6 copy-start.9
  1123.6 2.6 copy-start.10
  1123.6 2.7 copy-start.11
  1123.6 3.1 copy-start.6
Sparse Core Ops, SparseCore 0:
  1135.1 134.6 reduce-scatter.3
where the time goes:
time: 1290 us; the launch traced here: 1280 us
  other arithmetic  432 us (33%)
  loops' own time  289 us (22%)
  local copies, waits for them, and re-layouts  264 us (20%)
  waiting for transfers between devices  203 us (16%)
  between operations  53.1 us (4%)
  matrix products  18.8 us (1%)
  starting transfers between devices  17 us (1%)
    another operation x2, loops' own time, inverse_of(): lax.linalg.tridiagonal_solve(lower, middle, upper, jnp.eye(count, dtype=j...  289 us
    div x8, other arithmetic, inverse_of(): lax.linalg.tridiagonal_solve(lower, middle, upper, jnp.eye(count, dtype=j...  161 us
    sub x8, other arithmetic, inverse_of(): lax.linalg.tridiagonal_solve(lower, middle, upper, jnp.eye(count, dtype=j...  157 us
    unnamed x2, waiting for transfers between devices  135 us
    all_to_all x1, waiting for transfers between devices, transposed_x(): return lax.all_to_all(solved, 'gx', split_axis=1, concat_axis=2, tiled=True)  67.9 us
    unnamed x54, local copies, waits for them, and re-layouts  38.1 us
    slice x85, local copies, waits for them, and re-layouts, inverse_of(): lax.linalg.tridiagonal_solve(lower, middle, upper, jnp.eye(count, dtype=j...  37.6 us
    add x1, other arithmetic, explicit_y(): 0.75 * (take(1) - take(-1)) - 0.15 * (take(2) - take(-2))  35.8 us
  transfers between devices with their start and end apart: 5, of which 2 were waited for; matrix products, arithmetic and copies ran while one was open for 41% of the time, Pallas kernels for 0%

commit v1 on v0

--- a/solution.py
+++ b/solution.py
@@ -7,6 +7,12 @@
 time_step = 0.25
 four_pi = 4.0 * 3.141592653589793
 highest = lax.Precision.HIGHEST
+
+
+def swap_blocks(x, name, split, join):
+    pieces = jnp.split(x, lax.axis_size(name), axis=split)
+    received = lax.all_to_all(jnp.stack(pieces), name, 0, 0)
+    return jnp.concatenate(received, axis=join)
 
 
 def extended(block, sides, width):
@@ -81,7 +87,7 @@
     inverse = inverse_of(*diagonals(part.shape[1]))
     rhs = compact_rhs(part, 1)
     solved = jnp.einsum("ij,fjab->fiab", inverse, rhs, precision=highest)
-    return lax.all_to_all(solved, "gx", split_axis=1, concat_axis=2, tiled=True)
+    return swap_blocks(solved, "gx", 1, 2)
 
 
 def per_device(state, mean_flow, face_cell, face_normal, face_pos, observer_pos, time_bin):

time: 1290 us -> 1190 us (0.922)
  waiting for transfers between devices: 203 us -> 147 us
  local copies, waits for them, and re-layouts: 264 us -> 222 us
    all_to_all x1, waiting for transfers between devices: 67.9 us -> 11.7 us  [swap_blocks(): received = lax.all_to_all(jnp.stack(pieces), name, 0, 0)]
    slice x2, local copies, waits for them, and re-layouts: 33.4 us -> 19.9 us  [take(): return lax.slice_in_dim(padded, first, last, axis=axis)]
    all_to_all x2 -> x1, local copies, waits for them, and re-layouts: 16.9 us -> 4.01 us  [transposed_x(): part = lax.all_to_all(fields, 'gx', split_axis=2, concat_axis=1, tiled=True)]
    unnamed x54 -> x47, local copies, waits for them, and re-layouts: 38.1 us -> 45 us
  transfers between devices with their start and end apart: 5 -> 5, of which waited for: 2 -> 2; matrix products, arithmetic and copies ran while one was open for 41% -> 44% of each run, Pallas kernels for 0% -> 0%
where the time goes in v1:
time: 1190 us; the launch traced here: 1170 us
  other arithmetic  429 us (36%)
  loops' own time  285 us (24%)
  local copies, waits for them, and re-layouts  222 us (19%)
  waiting for transfers between devices  147 us (12%)
  between operations  53.4 us (4%)
  matrix products  18.5 us (2%)
  starting transfers between devices  16.9 us (1%)
    another operation x2, loops' own time, inverse_of(): lax.linalg.tridiagonal_solve(lower, middle, upper, jnp.eye(count, dtype=j...  285 us
    sub x8, other arithmetic, inverse_of(): lax.linalg.tridiagonal_solve(lower, middle, upper, jnp.eye(count, dtype=j...  159 us
    div x8, other arithmetic, inverse_of(): lax.linalg.tridiagonal_solve(lower, middle, upper, jnp.eye(count, dtype=j...  157 us
    unnamed x2, waiting for transfers between devices  135 us
    unnamed x47, local copies, waits for them, and re-layouts  45 us
    slice x85, local copies, waits for them, and re-layouts, inverse_of(): lax.linalg.tridiagonal_solve(lower, middle, upper, jnp.eye(count, dtype=j...  37.5 us
    concatenate x2, local copies, waits for them, and re-layouts, compact_rhs(): jnp.concatenate([first_row, second_row, middle_rows, before_last, last_ro...  36.3 us
    add x1, other arithmetic, explicit_y(): 0.75 * (take(1) - take(-1)) - 0.15 * (take(2) - take(-2))  35.8 us
  transfers between devices with their start and end apart: 5, of which 2 were waited for; matrix products, arithmetic and copies ran while one was open for 44% of the time, Pallas kernels for 0%

profile of v1, /device:TPU:0, one launch (start us, length us, event | category | flops | bytes accessed | tf_op | source)
XLA Modules:
  0.0 1172.3 jit_solution(3135238520413668037)
XLA Ops:
  30.5 446.5 %while.8 = (s32[]{:T(128)}, f32[]{:T(128)}, f32[256]{0:T(256)S(1)}, f32[7,32]{1,0:T(8,128)S(1)}, f32[7,32,256]{2,1,0:T(8,128)S(1)}, /*index=5*/f32[7,32]{1,0:T(8...) while((s32[]{:T(128)}, f32[]{:T(128)}, ...), condition=%wide.region_1.2_spmd, body=%wide.region_0.1_spmd.sunk | while | flops 24705 | bytes 269049 | solution.py:48
  73.8 19.7 %subtract_divide_fusion.125 = (f32[256]{0:T(256)S(1)}, f32[256]{0:T(256)S(1)}, f32[256]{0:T(256)S(1)}, f32[256]{0:T(256)S(1)}, f32[256]{0:T(256)S(1)}, /*index=5...) fusion(f32[256]{0:T(256)S(1)} %bitcast.1222, ...), kind=kLoop, calls=%fused_computation.37.clone.1 | loop fusion | flops 24576 | bytes 66816 | tf_op jit(solution)/shard_map/while/body/eval_jaxpr/div | solution.py:48
  137.6 19.7 %subtract_divide_fusion.125 = (f32[256]{0:T(256)S(1)}, f32[256]{0:T(256)S(1)}, f32[256]{0:T(256)S(1)}, f32[256]{0:T(256)S(1)}, f32[256]{0:T(256)S(1)}, /*index=5...) fusion(f32[256]{0:T(256)S(1)} %bitcast.1222, ...), kind=kLoop, calls=%fused_computation.37.clone.1 | loop fusion | flops 24576 | bytes 66816 | tf_op jit(solution)/shard_map/while/body/eval_jaxpr/div | solution.py:48
  201.4 19.7 %subtract_divide_fusion.125 = (f32[256]{0:T(256)S(1)}, f32[256]{0:T(256)S(1)}, f32[256]{0:T(256)S(1)}, f32[256]{0:T(256)S(1)}, f32[256]{0:T(256)S(1)}, /*index=5...) fusion(f32[256]{0:T(256)S(1)} %bitcast.1222, ...), kind=kLoop, calls=%fused_computation.37.clone.1 | loop fusion | flops 24576 | bytes 66816 | tf_op jit(solution)/shard_map/while/body/eval_jaxpr/div | solution.py:48
  265.1 19.7 %subtract_divide_fusion.125 = (f32[256]{0:T(256)S(1)}, f32[256]{0:T(256)S(1)}, f32[256]{0:T(256)S(1)}, f32[256]{0:T(256)S(1)}, f32[256]{0:T(256)S(1)}, /*index=5...) fusion(f32[256]{0:T(256)S(1)} %bitcast.1222, ...), kind=kLoop, calls=%fused_computation.37.clone.1 | loop fusion | flops 24576 | bytes 66816 | tf_op jit(solution)/shard_map/while/body/eval_jaxpr/div | solution.py:48
  328.9 19.7 %subtract_divide_fusion.125 = (f32[256]{0:T(256)S(1)}, f32[256]{0:T(256)S(1)}, f32[256]{0:T(256)S(1)}, f32[256]{0:T(256)S(1)}, f32[256]{0:T(256)S(1)}, /*index=5...) fusion(f32[256]{0:T(256)S(1)} %bitcast.1222, ...), kind=kLoop, calls=%fused_computation.37.clone.1 | loop fusion | flops 24576 | bytes 66816 | tf_op jit(solution)/shard_map/while/body/eval_jaxpr/div | solution.py:48
  392.7 19.7 %subtract_divide_fusion.125 = (f32[256]{0:T(256)S(1)}, f32[256]{0:T(256)S(1)}, f32[256]{0:T(256)S(1)}, f32[256]{0:T(256)S(1)}, f32[256]{0:T(256)S(1)}, /*index=5...) fusion(f32[256]{0:T(256)S(1)} %bitcast.1222, ...), kind=kLoop, calls=%fused_computation.37.clone.1 | loop fusion | flops 24576 | bytes 66816 | tf_op jit(solution)/shard_map/while/body/eval_jaxpr/div | solution.py:48
  456.5 19.7 %subtract_divide_fusion.125 = (f32[256]{0:T(256)S(1)}, f32[256]{0:T(256)S(1)}, f32[256]{0:T(256)S(1)}, f32[256]{0:T(256)S(1)}, f32[256]{0:T(256)S(1)}, /*index=5...) fusion(f32[256]{0:T(256)S(1)} %bitcast.1222, ...), kind=kLoop, calls=%fused_computation.37.clone.1 | loop fusion | flops 24576 | bytes 66816 | tf_op jit(solution)/shard_map/while/body/eval_jaxpr/div | solution.py:48
  518.1 19.1 %subtract_divide_fusion.32 = (f32[256]{0:T(256)S(1)}, f32[256]{0:T(256)S(1)}, f32[256]{0:T(256)S(1)}, f32[256]{0:T(256)S(1)}, f32[256]{0:T(256)S(1)}, /*index=5*...) fusion(f32[256]{0:T(256)S(1)} %bitcast.1441, ...), kind=kLoop, calls=%fused_computation.321 | loop fusion | flops 23808 | bytes 64760 | tf_op jit(solution)/shard_map/eval_jaxpr/div | solution.py:48
  539.8 151.9 %while.9 = (s32[]{:T(128)}, f32[256]{0:T(256)S(1)}, f32[7,32,256]{2,1,0:T(8,128)S(1)}, f32[7,32,256]{2,1,0:T(8,128)S(1)}, f32[7,32]{1,0:T(8,128)S(1)}, /*index=5...) while((s32[]{:T(128)}, f32[256]{0:T(256)S(1)}, ...), condition=%wide.region_3.4_spmd, body=%wide.region_2.3_spmd.sunk | while | flops 16418 | bytes 266721 | solution.py:48
  541.4 19.9 %multiply_subtract_fusion.125 = (f32[256]{0:T(256)S(1)}, f32[256]{0:T(256)S(1)}, f32[256]{0:T(256)S(1)}, f32[256]{0:T(256)S(1)}, f32[256]{0:T(256)S(1)}, /*index...) fusion(f32[256]{0:T(256)S(1)} %bitcast.1289, ...), kind=kLoop, calls=%fused_computation.103.clone.1 | loop fusion | flops 16384 | bytes 66688 | tf_op jit(solution)/shard_map/while/body/eval_jaxpr/sub | solution.py:48
  563.1 19.9 %multiply_subtract_fusion.125 = (f32[256]{0:T(256)S(1)}, f32[256]{0:T(256)S(1)}, f32[256]{0:T(256)S(1)}, f32[256]{0:T(256)S(1)}, f32[256]{0:T(256)S(1)}, /*index...) fusion(f32[256]{0:T(256)S(1)} %bitcast.1289, ...), kind=kLoop, calls=%fused_computation.103.clone.1 | loop fusion | flops 16384 | bytes 66688 | tf_op jit(solution)/shard_map/while/body/eval_jaxpr/sub | solution.py:48
  584.8 19.9 %multiply_subtract_fusion.125 = (f32[256]{0:T(256)S(1)}, f32[256]{0:T(256)S(1)}, f32[256]{0:T(256)S(1)}, f32[256]{0:T(256)S(1)}, f32[256]{0:T(256)S(1)}, /*index...) fusion(f32[256]{0:T(256)S(1)} %bitcast.1289, ...), kind=kLoop, calls=%fused_computation.103.clone.1 | loop fusion | flops 16384 | bytes 66688 | tf_op jit(solution)/shard_map/while/body/eval_jaxpr/sub | solution.py:48
  606.6 19.9 %multiply_subtract_fusion.125 = (f32[256]{0:T(256)S(1)}, f32[256]{0:T(256)S(1)}, f32[256]{0:T(256)S(1)}, f32[256]{0:T(256)S(1)}, f32[256]{0:T(256)S(1)}, /*index...) fusion(f32[256]{0:T(256)S(1)} %bitcast.1289, ...), kind=kLoop, calls=%fused_computation.103.clone.1 | loop fusion | flops 16384 | bytes 66688 | tf_op jit(solution)/shard_map/while/body/eval_jaxpr/sub | solution.py:48
  628.3 19.9 %multiply_subtract_fusion.125 = (f32[256]{0:T(256)S(1)}, f32[256]{0:T(256)S(1)}, f32[256]{0:T(256)S(1)}, f32[256]{0:T(256)S(1)}, f32[256]{0:T(256)S(1)}, /*index...) fusion(f32[256]{0:T(256)S(1)} %bitcast.1289, ...), kind=kLoop, calls=%fused_computation.103.clone.1 | loop fusion | flops 16384 | bytes 66688 | tf_op jit(solution)/shard_map/while/body/eval_jaxpr/sub | solution.py:48
  650.0 19.9 %multiply_subtract_fusion.125 = (f32[256]{0:T(256)S(1)}, f32[256]{0:T(256)S(1)}, f32[256]{0:T(256)S(1)}, f32[256]{0:T(256)S(1)}, f32[256]{0:T(256)S(1)}, /*index...) fusion(f32[256]{0:T(256)S(1)} %bitcast.1289, ...), kind=kLoop, calls=%fused_computation.103.clone.1 | loop fusion | flops 16384 | bytes 66688 | tf_op jit(solution)/shard_map/while/body/eval_jaxpr/sub | solution.py:48
  671.7 19.9 %multiply_subtract_fusion.125 = (f32[256]{0:T(256)S(1)}, f32[256]{0:T(256)S(1)}, f32[256]{0:T(256)S(1)}, f32[256]{0:T(256)S(1)}, f32[256]{0:T(256)S(1)}, /*index...) fusion(f32[256]{0:T(256)S(1)} %bitcast.1289, ...), kind=kLoop, calls=%fused_computation.103.clone.1 | loop fusion | flops 16384 | bytes 66688 | tf_op jit(solution)/shard_map/while/body/eval_jaxpr/sub | solution.py:48
  691.7 19.3 %multiply_subtract_fusion.32 = (f32[256]{0:T(256)S(1)}, f32[256]{0:T(256)S(1)}, f32[256]{0:T(256)S(1)}, f32[256]{0:T(256)S(1)}, f32[256]{0:T(256)S(1)}, /*index=...) fusion(f32[256]{0:T(256)S(1)} %bitcast.1387, ...), kind=kLoop, calls=%fused_computation.290 | loop fusion | flops 15872 | bytes 64636 | tf_op jit(solution)/shard_map/eval_jaxpr/sub | solution.py:48
  715.4 11.8 %pad_slice_fusion.21 = (f32[5,256,6,256]{3,1,2,0:T(8,128)}, f32[5,256,6,256]{3,1,2,0:T(8,128)}, f32[5,256,6,256]{3,1,2,0:T(8,128)}, f32[5,256,6,256]{3,1,2,0:T(8,128)}) fusion(f32[5,256,6,256]{3,1,2,0:T(8,128)S(1)} %bitcast.1153), kind=kLoop, calls=%fused_computation.165 | loop fusion | bytes 39321600 | tf_op jit(solution)/shard_map/slice | solution.py:57
  727.1 15.4 %fusion.1 = f32[5,252,6,256]{3,1,2,0:T(8,128)} fusion(f32[5,256,6,256]{3,1,2,0:T(8,128)} %get-tuple-element.519, f32[5,256,6,256]{3,1,2,0:T(8,128)} %get-tuple-element.521, f32[5,256,6,256]{3,1,2,0:T(8,128)} %get-tuple-element.520, f32[5,256,6,256]{3,1,2,0:T(8,128)} %get-tuple-element.518), kind=kLoop, calls=%fused_computation.153 | loop fusion | flops 9676800 | bytes 38707200 | tf_op jit(solution)/shard_map/add | solution.py:62
  742.5 24.6 %concatenate.55 = f32[5,256,6,256]{3,1,2,0:T(8,128)} concatenate(f32[5,1,6,256]{3,1,2,0:T(1,128)S(1)} %get-tuple-element.517, f32[5,1,6,256]{3,1,2,0:T(1,128)S(1)} %get-tuple-element.516, f32[5,252,6,256]{3,1,2,0:T(8,128)} %fusion.1, f32[5,1,6,256]{3,1,2,0:T(1,128)S(1)} %get-tuple-element.515, f32[5,1,6,256]{3,1,2,0:T(1,128)S(1)} %get-tuple-element.514), dimensions={1} | concatenate | bytes 15728640 | tf_op jit(solution)/shard_map/concatenate | solution.py:70
  767.1 10.1 convolution_bitcast_fusion
  849.4 9.6 fusion.5
  859.0 11.7 concatenate.62
  882.0 8.8 constant_dynamic-update-slice_fusion.1
  892.5 11.5 fusion.77
  904.0 11.4 fusion.76
  915.4 35.8 %fusion.8 = f32[3,32,48,256]{3,2,1,0:T(8,128)} fusion(f32[3,32,48,256]{3,1,2,0:T(8,128)} %get-tuple-element.529, f32[3,32,48,256]{3,1,2,0:T(8,128)} %get-tuple-element.526, f32[3,32,48,256]{3,1,2,0:T(8,128)} %get-tuple-element.528, f32[3,32,48,256]{3,1,2,0:T(8,128)} %get-tuple-element.525, f32[3,32,48,256]{3,1,2,0:T(8,128)} %get-tuple-element.527, ...), kind=kLoop, calls=%fused_computation.176 | loop fusion | flops 9437184 | bytes 33030144 | tf_op jit(solution)/shard_map/add | solution.py:79
  951.2 11.7 %all-to-all-done.1 = f32[8,5,32,6,256]{4,2,3,1,0:T(8,128)} async-done(((f32[8,5,32,6,256]{4,2,3,1,0:T(8,128)}), f32[8,5,32,6,256]{4,2,3,1,0:T(8,128)}, u32[]{:S(2)}, u32[]{:S(2)}) %all-to-all-start.1) | async-done | bytes 7864352 | tf_op jit(solution)/shard_map/all_to_all | solution.py:14
  968.1 13.1 %fusion.30 = (f32[32,48,256]{2,1,0:T(8,128)S(1)}, f32[32,48,256]{2,1,0:T(8,128)S(1)}, f32[32,48,256]{2,1,0:T(8,128)}, f32[32,48,256]{2,1,0:T(8,128)}) fusion(f32[3,32,48,256]{3,2,1,0:T(8,128)} %fusion.50, f32[3,32,48,256]{3,2,1,0:T(8,128)S(1)} %copy-done.2, f32[32,48,256]{2,1,0:T(8,128)S(1)} %copy-done.5, f32[32,48,256]{2,0,1:T(8,128)S(1)} %bitcast.1164, ...), kind=kLoop, calls=%fused_computation.206 | loop fusion | flops 7864320 | bytes 29884416 | tf_op jit(solution)/shard_map/neg | solution.py:103
  1007.8 8.6 pad_maximum_fusion.2
  1030.4 134.9 %reduce-scatter.4.cloned.1.call-done = f32[16,64]{1,0:T(8,128)} async-done(((f32[512,64]{1,0:T(8,128)}), f32[16,64]{1,0:T(8,128)}) %reduce-scatter.4.cloned.1.call-update) | async-done | bytes 4112
  (261 shorter events, 198.7 us)
Async XLA Ops:
  11.1 3.1 copy-start
  21.9 689.3 %all-to-all-start = ((f32[5,32,48,256]{3,1,0,2:T(8,128)}), f32[5,32,48,256]{3,1,0,2:T(8,128)}, u32[]{:S(2)}, u32[]{:S(2)}) async-start(f32[5,32,48,256]{3,1,0,2:T(8,128)} %copy.115), calls=%async_computation | async-start | bytes 15728640 | tf_op jit(solution)/shard_map/all_to_all | solution.py:86
  785.6 177.4 %all-to-all-start.1 = ((f32[8,5,32,6,256]{4,2,3,1,0:T(8,128)}), f32[8,5,32,6,256]{4,2,3,1,0:T(8,128)}, u32[]{:S(2)}, u32[]{:S(2)}) async-start(f32[8,5,32,6,256]{4,2,3,1,0:T(8,128)} %fusion.33), calls=%async_computation.1 | async-start | bytes 15728640 | tf_op jit(solution)/shard_map/all_to_all | solution.py:14
  791.6 373.7 %reduce-scatter.4.cloned.1.call-start = ((), (), s32[]{:S(2)}) async-start(), calls=%async_computation.3 | async-start | bytes 270336
  794.3 6.6 copy-start.1
  794.3 6.7 copy-start.4
  795.2 85.1 %collective-permute-start.1 = (f32[3,32,3,256]{3,1,2,0:T(8,128)}, f32[3,32,3,256]{3,1,2,0:T(8,128)}, u32[]{:S(2)}, u32[]{:S(2)}) collective-permute-start(f32[3,32,3,256]{3,1,2,0:T(8,128)} %copy.194), channel_id=1, source_target_pairs={{0,1},{1,2},{2,3},{4,5},{5,6},{6,7},{8,9},{9,10},{10,11},{12,13},{... | collective-permute-start | bytes 884744 | tf_op jit(solution)/shard_map/ppermute | solution.py:23
  798.1 92.7 %collective-permute-start = (f32[3,32,3,256]{3,1,2,0:T(8,128)}, f32[3,32,3,256]{3,1,2,0:T(8,128)}, u32[]{:S(2)}, u32[]{:S(2)}) collective-permute-start(f32[3,32,3,256]{3,1,2,0:T(8,128)} %copy.195), channel_id=1, source_target_pairs={{1,0},{2,1},{3,2},{5,4},{6,5},{7,6},{9,8},{10,9},{11,10},{13,12},{... | collective-permute-start | bytes 884744 | tf_op jit(solution)/shard_map/ppermute | solution.py:26
  800.9 2.2 copy-start.3
  859.0 11.7 copy-start.13
  859.0 11.8 %copy-start.11 = (f32[3,192]{1,0:T(4,128)S(1)}, f32[3,192]{1,0:T(4,128)}, u32[]{:S(2)}) copy-start(f32[3,192]{1,0:T(4,128)} %param.14) | copy-start | bytes 6916
  859.0 11.8 %copy-start.12 = (f32[3,192]{1,0:T(4,128)S(1)}, f32[3,192]{1,0:T(4,128)}, u32[]{:S(2)}) copy-start(f32[3,192]{1,0:T(4,128)} %param.15) | copy-start | bytes 6916
  871.4 8.4 copy-start.10
  962.9 4.7 copy-start.2
  962.9 5.2 copy-start.5
  999.6 2.7 copy-start.6
  1002.3 5.5 copy-start.7
  1002.3 5.5 copy-start.8
  1007.8 14.3 %copy-start.9 = (s32[192,512]{1,0:T(8,128)S(1)}, s32[192,512]{1,0:T(8,128)}, u32[]{:S(2)}) copy-start(s32[192,512]{1,0:T(8,128)} %param.17) | copy-start | bytes 1179652
Sparse Core Ops, SparseCore 0:
  1030.5 134.6 reduce-scatter.3
